TPU v7x, 8 devices: a whole 2x2x1 slice. The times are simulated.
8 devices in a mesh: depth: 2 (over z, y), col: 2 (over x), row: 2 (over core).
Axes of the slice: x: 2, y: 2, z: 1, core: 2. Of those that a mesh axis runs over, the one named last changes fastest.
Arguments:
- a_mat: bfloat16 [4096, 4096], P(('row', 'depth'), 'col')
- b_mat: bfloat16 [4096, 4096], P(('row', 'depth'), 'col')
Outputs:
- output: bfloat16 [4096, 4096], P(('row', 'depth'), 'col')
All inputs are finite; a program needn't handle non-finite values.
Results may differ from a plain program's by a relative error of at most 0.001.
Values are sent between devices in bfloat16 or wider.
A program may use at most 1 GiB of HBM per device.

v0:
```python
import jax
import jax.numpy as jnp
from jax import lax
from jax.sharding import PartitionSpec as P, NamedSharding


def solution(mesh):
    depth_n = mesh.shape["depth"]
    col_n = mesh.shape["col"]
    row_n = mesh.shape["row"]
    row_ratio = row_n // col_n
    layer_steps = row_n // depth_n
    all_axes = ("depth", "col", "row")

    def linear(layer, col_idx, row_idx):
        return (layer * col_n + col_idx) * row_n + row_idx

    def first_k(layer, row_idx):
        return (row_idx + layer * layer_steps) % row_n

    b_start = [
        (linear(layer, col_idx, (first_k(layer, row_idx) + col_idx * row_ratio) % row_n), linear(layer, col_idx, row_idx))
        for layer in range(depth_n) for col_idx in range(col_n) for row_idx in range(row_n)
    ]
    a_start = [
        (linear(layer, (col_idx + first_k(layer, row_idx) // row_ratio) % col_n, row_idx), linear(layer, col_idx, row_idx))
        for layer in range(depth_n) for col_idx in range(col_n) for row_idx in range(row_n)
    ]
    a_after = [
        (linear(layer, (col_idx + first_k(layer, row_idx) // row_ratio + 1) % col_n, row_idx), linear(layer, col_idx, row_idx))
        for layer in range(depth_n) for col_idx in range(col_n) for row_idx in range(row_n)
    ]
    b_shift = [((row_idx + 1) % row_n, row_idx) for row_idx in range(row_n)]
    a_shift = [((col_idx + 1) % col_n, col_idx) for col_idx in range(col_n)]

    def local_product(a_blk, b_blk):
        a_full = lax.all_gather(a_blk, "depth", axis=0, tiled=True)
        b_full = lax.all_gather(b_blk, "depth", axis=0, tiled=True)
        piece_w = a_full.shape[0]
        col_w = a_full.shape[1]
        b_cur = lax.ppermute(b_full, all_axes, b_start)
        a_lead = lax.ppermute(a_full, all_axes, a_start)
        if row_ratio == 1:
            queue = a_lead
        else:
            a_tail = lax.ppermute(a_full, all_axes, a_after)
            offset = (lax.axis_index("row") + lax.axis_index("depth") * layer_steps) % row_n % row_ratio
            joined = jnp.concatenate([a_lead, a_tail], axis=1)
            queue = lax.dynamic_slice_in_dim(joined, offset * piece_w, col_w, axis=1)
        pieces = [queue[:, slot * piece_w:(slot + 1) * piece_w] for slot in range(min(row_ratio, layer_steps))]
        part_sum = jnp.dot(pieces[0], b_cur, preferred_element_type=jnp.float32)
        for step in range(1, layer_steps):
            if step - 1 + row_ratio < layer_steps:
                pieces = pieces[1:] + [lax.ppermute(pieces[0], "col", a_shift)]
            else:
                pieces = pieces[1:]
            b_cur = lax.ppermute(b_cur, "row", b_shift)
            part_sum = part_sum + jnp.dot(pieces[0], b_cur, preferred_element_type=jnp.float32)
        c_part = lax.psum_scatter(part_sum, "depth", scatter_dimension=0, tiled=True)
        return c_part.astype(jnp.bfloat16)

    block_spec = P(("row", "depth"), "col")
    return jax.shard_map(local_product, mesh=mesh, in_specs=(block_spec, block_spec), out_specs=block_spec, check_vma=False)
```

profile of v0, /device:TPU:0, one launch (start us, length us, event | category | flops | bytes accessed | tf_op | source)
XLA Modules:
  0.0 534.1 jit_solution(10361110063155470458)
XLA Ops:
  6.5 0.0 all-gather.5.cloned.1.call-start
  6.5 0.7 all-gather.5.cloned.1.call-update
  7.3 0.0 all-gather.3.cloned.1.call-start
  7.3 0.7 all-gather.3.cloned.1.call-update
  8.0 0.0 reduce-scatter.2.cloned.1.call-start
  8.1 105.9 %all-gather.5.cloned.1.call-done = bf16[2048,2048]{1,0:T(8,128)(2,1)} async-done(((bf16[1024,2048]{1,0:T(8,128)(2,1)}), bf16[2048,2048]{1,0:T(8,128)(2,1)}) %all-gather.5.cloned.1.call-update) | async-done | bytes 8388624 | tf_op jit(solution)/shard_map/all_gather | solution.py:38
  114.0 64.4 %collective-permute-start.1 = (bf16[2048,2048]{1,0:T(8,128)(2,1)}, bf16[2048,2048]{1,0:T(8,128)(2,1)}, u32[]{:S(2)}, u32[]{:S(2)}) collective-permute-start(bf16[2048,2048]{1,0:T(8,128)(2,1)} %all-gather.5.cloned.1.call-done), channel_id=1, source_target_pairs={{0,0},{1,1},{3,2},{2,3},{5,4},{4,5},{6,6},{7,7}} | collective-permute-start | bytes 25165832 | tf_op jit(solution)/shard_map/ppermute | solution.py:41
  178.4 39.4 %all-gather.3.cloned.1.call-done = bf16[2048,2048]{1,0:T(8,128)(2,1)} async-done(((bf16[1024,2048]{1,0:T(8,128)(2,1)}), bf16[2048,2048]{1,0:T(8,128)(2,1)}) %all-gather.3.cloned.1.call-update) | async-done | bytes 8388624 | tf_op jit(solution)/shard_map/all_gather | solution.py:37
  217.8 4.0 collective-permute-start
  221.8 0.0 collective-permute-done.1
  221.8 0.0 collective-permute-done
  221.8 21.9 %fusion = f32[2048,2048]{1,0:T(8,128)} fusion(bf16[2048,2048]{1,0:T(8,128)(2,1)S(1)} %collective-permute-done, bf16[2048,2048]{1,0:T(8,128)(2,1)} %collective-permute-done.1), kind=kOutput, calls=%fused_computation | convolution fusion | flops 17179869184 | bytes 33554432 | tf_op jit(solution)/shard_map/dot_general | solution.py:51
  243.7 0.0 reduce-scatter.2.cloned.1.call-update
  243.7 277.8 %reduce-scatter.2.cloned.1.call-done = f32[1024,2048]{1,0:T(8,128)} async-done(((f32[2048,2048]{1,0:T(8,128)}), f32[1024,2048]{1,0:T(8,128)}) %reduce-scatter.2.cloned.1.call-update) | async-done | bytes 8388624 | tf_op jit(solution)/shard_map/reduce_scatter | solution.py:59
  521.5 6.0 %convert_element_type.3 = bf16[1024,2048]{1,0:T(8,128)(2,1)} convert(f32[1024,2048]{1,0:T(8,128)} %reduce-scatter.2.cloned.1.call-done) | non-fusion elementwise | flops 2097152 | bytes 12582912 | tf_op jit(solution)/shard_map/convert_element_type | solution.py:60
Async XLA Ops:
  6.5 107.4 %all-gather.5.cloned.1.call-start = ((), (), s32[]{:S(2)}) async-start(), calls=%async_computation.2 | async-start | bytes 12582912 | tf_op jit(solution)/shard_map/all_gather | solution.py:38
  7.3 210.5 %all-gather.3.cloned.1.call-start = ((), (), s32[]{:S(2)}) async-start(), calls=%async_computation.1 | async-start | bytes 12582912 | tf_op jit(solution)/shard_map/all_gather | solution.py:37
  8.0 513.5 %reduce-scatter.2.cloned.1.call-start = ((), (), s32[]{:S(2)}) async-start(), calls=%async_computation.3 | async-start | bytes 25165824 | tf_op jit(solution)/shard_map/reduce_scatter | solution.py:59
  114.0 107.8 %collective-permute-start.1 = (bf16[2048,2048]{1,0:T(8,128)(2,1)}, bf16[2048,2048]{1,0:T(8,128)(2,1)}, u32[]{:S(2)}, u32[]{:S(2)}) collective-permute-start(bf16[2048,2048]{1,0:T(8,128)(2,1)} %all-gather.5.cloned.1.call-done), channel_id=1, source_target_pairs={{0,0},{1,1},{3,2},{2,3},{5,4},{4,5},{6,6},{7,7}} | collective-permute-start | bytes 25165832 | tf_op jit(solution)/shard_map/ppermute | solution.py:41
  217.8 4.0 collective-permute-start
Sparse Core Ops, SparseCore 0:
  8.8 105.0 all-gather.4
  115.5 102.2 all-gather.2
  243.9 277.6 reduce-scatter.1
where the time goes:
time: 539 us; the launch traced here: 534 us
  waiting for transfers between devices  425 us (79%)
  starting transfers between devices  68.5 us (13%)
  matrix products  21.9 us (4%)
  between operations  13.1 us (2%)
  other arithmetic  6.05 us (1%)
    reduce_scatter x1, waiting for transfers between devices, local_product(): lax.psum_scatter(part_sum, 'depth', scatter_dimension=0, tiled=True)  278 us
    all_gather x1, waiting for transfers between devices, local_product(): b_full = lax.all_gather(b_blk, 'depth', axis=0, tiled=True)  106 us
    ppermute x1, starting transfers between devices, local_product(): b_cur = lax.ppermute(b_full, all_axes, b_start)  64.4 us
    all_gather x1, waiting for transfers between devices, local_product(): a_full = lax.all_gather(a_blk, 'depth', axis=0, tiled=True)  39.4 us
    dot_general x1, matrix products, local_product(): part_sum = jnp.dot(pieces[0], b_cur, preferred_element_type=jnp.float32)  21.9 us
  transfers between devices with their start and end apart: 5, of which 3 were waited for; matrix products, arithmetic and copies ran while one was open for 0% of the time, Pallas kernels for 0%

commit v1 on v0

v1 whole, which is shorter than its diff:
```python
import functools

import jax
import jax.numpy as jnp
from jax import lax
from jax.experimental import pallas as pl
from jax.experimental.pallas import tpu as pltpu
from jax.sharding import PartitionSpec as P

MESH = pl.DeviceIdType.MESH
BF16, F32 = jnp.bfloat16, jnp.float32

Q = 1024
ROWS, COLS = 1024, 2048

B_STEPS = [(0, 0, 256), (256, 256, 256), (512, 512, 256), (768, 768, 128), (960, 896, 64), (896, 960, 64)]
A_STEPS = [(3, 0, 512), (3, 512, 512), (2, 0, 512), (2, 512, 256), (2, 768, 128), (2, 896, 128)]
STEPS = len(B_STEPS)
LAST = STEPS - 1
TM, TN = 256, 512


def exchange_kernel(a_ref, b_ref, acc, alast, blast, a4, b4, apen, bpen,
                    la_sem, lb_sem, xs, xr, ys, yr, fs, ds, dr):
    dep, col, row = lax.axis_index("depth"), lax.axis_index("col"), lax.axis_index("row")
    x_nbr, y_nbr, sib = (dep, 1 - col, row), (1 - dep, col, row), (dep, col, 1 - row)
    pair = (row + col) % 2
    other = 1 - pair
    near = pl.multiple_of(dep * Q, Q)
    far = pl.multiple_of((1 - dep) * Q, Q)

    load_a = [
        pltpu.make_async_copy(a_ref.at[:, pl.ds(near, Q)], a4.at[0], la_sem.at[0]),
        pltpu.make_async_copy(a_ref.at[:, pl.ds(far, Q)], a4.at[1], la_sem.at[1]),
    ]
    load_b = pltpu.make_async_copy(b_ref, b4.at[2 * pair], lb_sem)

    barrier = pltpu.get_barrier_semaphore()
    for dev in (x_nbr, y_nbr, sib):
        pl.semaphore_signal(barrier, inc=1, device_id=dev, device_id_type=MESH)
    for copy in load_a:
        copy.start()
    load_b.start()
    pl.semaphore_wait(barrier, 3)

    def a_copy(step):
        slot, start, size = A_STEPS[step]
        src = a_ref.at[:, pl.ds(pl.multiple_of((near if slot == 2 else far) + start, 128), size)]
        dst = alast.at[:, pl.ds(0, 128)] if step == LAST else a4.at[slot, :, pl.ds(start, size)]
        return pltpu.make_async_remote_copy(src, dst, xs.at[step], xr.at[step], device_id=x_nbr, device_id_type=MESH)

    def b_place(step, which):
        s1, s3, size = B_STEPS[step]
        if step == LAST:
            return blast.at[pl.ds(pl.multiple_of(128 + which * 64, 64), size)]
        if step == LAST - 1:
            return bpen.at[pl.ds(pl.multiple_of((1 - which) * 64, 64), size)]
        return b4.at[2 * which + 1, pl.ds(s1, size)]

    def b_start(step, which):
        s1, s3, _ = B_STEPS[step]
        return pl.multiple_of(s1 + which * (s3 - s1), 64)

    def b_copy(step):
        size = B_STEPS[step][2]
        return pltpu.make_async_remote_copy(
            b_ref.at[pl.ds(b_start(step, pair), size)], b_place(step, pair), ys.at[step], yr.at[pair, step],
            device_id=y_nbr, device_id_type=MESH)

    def forward(step):
        return pltpu.make_async_remote_copy(
            b_place(step, pair), b_place(step, pair), fs.at[step], yr.at[pair, step],
            device_id=sib, device_id_type=MESH)

    def forwarded(step):
        return pltpu.make_async_remote_copy(
            b_place(step, other), b_place(step, other), fs.at[step], yr.at[other, step],
            device_id=sib, device_id_type=MESH)

    give = pltpu.make_async_remote_copy(b_ref, b4.at[2 * pair], ds, dr, device_id=sib, device_id_type=MESH)
    take = pltpu.make_async_remote_copy(b_ref, b4.at[2 * other], ds, dr, device_id=sib, device_id_type=MESH)

    for step in range(STEPS):
        a_copy(step).start()
        b_copy(step).start()
        if step == 0:
            give.start()

    def multiply(a_view, b_view, fresh=False):
        @pl.loop(0, (ROWS // TM) * (COLS // TN))
        def _(t):
            rows = pl.ds(pl.multiple_of((t // (COLS // TN)) * TM, TM), TM)
            cols = pl.ds(pl.multiple_of((t % (COLS // TN)) * TN, TN), TN)
            part = jnp.dot(a_view(rows), b_view(cols), preferred_element_type=F32)
            if fresh:
                acc[rows, cols] = part
            else:
                acc[rows, cols] += part

    def slot_product(slot, start, size, fresh=False):
        multiply(lambda r: a4[slot, r, pl.ds(start, size)], lambda c: b4[slot, pl.ds(start, size), c], fresh)

    for copy in load_a:
        copy.wait()
    load_b.wait()
    give.wait_send()
    take.wait_recv()
    slot_product(0, 0, Q, fresh=True)
    blast[pl.ds(0, 128), :] = b4[2, pl.ds(Q - 128, 128), :]

    for step in range(STEPS):
        b_copy(step).wait_recv()
        forward(step).start()
        a_copy(step).wait_recv()
        if step == 1:
            low = lax.broadcasted_iota(jnp.int32, (TM, 128), 1) < 64

            @pl.loop(0, ROWS // TM)
            def _(t):
                rows = pl.ds(pl.multiple_of(t * TM, TM), TM)
                a1, a3 = a4[1, rows, pl.ds(Q - 128, 128)], a4[3, rows, pl.ds(Q - 128, 128)]
                apen[rows, :] = jnp.where(low, a3, a1)
                alast[rows, pl.ds(128, 128)] = jnp.where(low, a1, a3)
        slot, start, size = A_STEPS[step]
        if slot == 2 and step != LAST:
            slot_product(2, start, size)
        forwarded(step).wait_recv()
        if step < LAST - 1:
            slot_product(1, B_STEPS[step][0], B_STEPS[step][2])
            slot_product(3, B_STEPS[step][1], B_STEPS[step][2])
        elif step == LAST - 1:
            multiply(lambda r: apen[r, :], lambda c: bpen[:, c])

    for step in range(STEPS):
        a_copy(step).wait_send()
        b_copy(step).wait_send()
        forward(step).wait_send()


def finish_kernel(acc, alast, blast, c_ref, stage, sem):
    blk = 128
    copies = []
    for t in range(ROWS // blk):
        rows = pl.ds(t * blk, blk)
        tail = jnp.dot(alast[rows, :], blast[...], preferred_element_type=F32)
        stage[rows, :] = (acc[rows, :] + tail).astype(BF16)
        copies.append(pltpu.make_async_copy(stage.at[rows], c_ref.at[rows], sem.at[t]))
        copies[-1].start()
    for copy in copies:
        copy.wait()


def solution(mesh):
    hbm = pl.BlockSpec(memory_space=pltpu.HBM)
    vmem = pl.BlockSpec(memory_space=pltpu.VMEM)
    dma = pltpu.SemaphoreType.DMA

    def local_product(a_blk, b_blk):
        a_blk = pltpu.with_memory_space_constraint(a_blk, pltpu.HBM)
        b_blk = pltpu.with_memory_space_constraint(b_blk, pltpu.HBM)
        acc, alast, blast = pl.pallas_call(
            exchange_kernel,
            out_shape=(
                pltpu.VMEM((ROWS, COLS), F32),
                pltpu.VMEM((ROWS, 256), BF16),
                pltpu.VMEM((256, COLS), BF16),
            ),
            in_specs=[hbm, hbm],
            out_specs=(vmem, vmem, vmem),
            scratch_shapes=[
                pltpu.VMEM((4, ROWS, Q), BF16),
                pltpu.VMEM((4, Q, COLS), BF16),
                pltpu.VMEM((ROWS, 128), BF16),
                pltpu.VMEM((128, COLS), BF16),
                dma((2,)), dma, dma((STEPS,)), dma((STEPS,)), dma((STEPS,)), dma((2, STEPS)), dma((STEPS,)), dma, dma,
            ],
            compiler_params=pltpu.CompilerParams(
                collective_id=0, has_side_effects=True, vmem_limit_bytes=44 * 2**20),
            name="exchange",
        )(a_blk, b_blk)
        return pl.pallas_call(
            finish_kernel,
            out_shape=pltpu.HBM((ROWS, COLS), BF16),
            in_specs=[vmem, vmem, vmem],
            out_specs=hbm,
            scratch_shapes=[pltpu.VMEM((ROWS, COLS), BF16), dma((8,))],
            compiler_params=pltpu.CompilerParams(vmem_limit_bytes=24 * 2**20),
            name="finish",
        )(acc, alast, blast)

    spec = P(("row", "depth"), "col")
    return jax.shard_map(local_product, mesh=mesh, in_specs=(spec, spec), out_specs=spec, check_vma=False)
```

time: 539 us -> 108 us (0.20)
  waiting for transfers between devices: 425 us -> 0 us
  Pallas kernels: 0 us -> 108 us
  starting transfers between devices: 68.5 us -> 0 us
  matrix products: 21.9 us -> 0 us
  between operations: 13.1 us -> 0.01 us
  other arithmetic: 6.05 us -> 0 us
    reduce_scatter x1 -> x0, waiting for transfers between devices: 278 us -> none  [local_product(): lax.psum_scatter(part_sum, 'depth', scatter_dimension=0, tiled=True)]
    all_gather x2 -> x0, waiting for transfers between devices: 145 us -> none  [the longest x1 106 us: local_product(): b_full = lax.all_gather(b_blk, 'depth', axis=0, tiled=True)]
    pallas_call x0 -> x2, Pallas kernels: none -> 108 us  [the longest x1 106 us: local_product(): pl.pallas_call(exchange_kernel, out_shape=(pltpu.VMEM((ROWS, COLS), F32),...]
    ppermute x2 -> x0, starting transfers between devices: 68.4 us -> none  [the longest x1 64.4 us: local_product(): b_cur = lax.ppermute(b_full, all_axes, b_start)]
    dot_general x1 -> x0, matrix products: 21.9 us -> none  [local_product(): part_sum = jnp.dot(pieces[0], b_cur, preferred_element_type=jnp.float32)]
    convert_element_type x1 -> x0, other arithmetic: 6.05 us -> none  [local_product(): return c_part.astype(jnp.bfloat16)]
  transfers between devices with their start and end apart: 5 -> 0, of which waited for: 3 -> 0; matrix products, arithmetic and copies ran while one was open for 0% -> 0% of each run, Pallas kernels for 0% -> 0%
where the time goes in v1:
time: 108 us
  Pallas kernels  108 us (100%)
    pallas_call x1, Pallas kernels, local_product(): pl.pallas_call(exchange_kernel, out_shape=(pltpu.VMEM((ROWS, COLS), F32),...  106 us
    pallas_call x1, Pallas kernels, local_product(): pl.pallas_call(finish_kernel, out_shape=pltpu.HBM((ROWS, COLS), BF16), in...  2.39 us

profile of v1, /device:TPU:0, one launch (start us, length us, event | category | flops | bytes accessed | tf_op | source)
XLA Modules:
  0.0 108.1 jit_solution(5993048428967942905)
XLA Ops:
  0.0 105.7 %exchange.1 = (f32[1024,2048]{1,0:T(8,128)S(1)}, bf16[1024,256]{1,0:T(8,128)(2,1)S(1)}, bf16[256,2048]{1,0:T(8,128)(2,1)S(1)}) custom-call(bf16[1024,2048]{1,0:T(8,128)(2,1)} %a_ref.1, bf16[1024,2048]{1,0:T(8,128)(2,1)} %b_ref.1), custom_call_target="tpu_custom_call" | custom-call | tf_op jit(solution)/shard_map/exchange/pallas_call | solution.py:161
  105.7 2.4 %finish.1 = bf16[1024,2048]{1,0:T(8,128)(2,1)} custom-call(f32[1024,2048]{1,0:T(8,128)S(1)} %get-tuple-element.8.acc, bf16[1024,256]{1,0:T(8,128)(2,1)S(1)} %get-tuple-element.9.alast, bf16[256,2048]{1,0:T(8,128)(2,1)S(1)} %get-tuple-element.10.blast), custom_call_target="tpu_custom_call" | custom-call | tf_op jit(solution)/shard_map/finish/pallas_call | solution.py:181

commit v2 on v1

--- a/solution.py
+++ b/solution.py
@@ -17,11 +17,11 @@
 A_STEPS = [(3, 0, 512), (3, 512, 512), (2, 0, 512), (2, 512, 256), (2, 768, 128), (2, 896, 128)]
 STEPS = len(B_STEPS)
 LAST = STEPS - 1
-TM, TN = 256, 512
+TM, TN = 512, 1024
 
 
 def exchange_kernel(a_ref, b_ref, acc, alast, blast, a4, b4, apen, bpen,
-                    la_sem, lb_sem, xs, xr, ys, yr, fs, ds, dr):
+                    ready, la_sem, lb_sem, xs, xr, ys, yr, fs, ds, dr):
     dep, col, row = lax.axis_index("depth"), lax.axis_index("col"), lax.axis_index("row")
     x_nbr, y_nbr, sib = (dep, 1 - col, row), (1 - dep, col, row), (dep, col, 1 - row)
     pair = (row + col) % 2
@@ -36,12 +36,18 @@
     load_b = pltpu.make_async_copy(b_ref, b4.at[2 * pair], lb_sem)
 
     barrier = pltpu.get_barrier_semaphore()
-    for dev in (x_nbr, y_nbr, sib):
-        pl.semaphore_signal(barrier, inc=1, device_id=dev, device_id_type=MESH)
-    for copy in load_a:
-        copy.start()
-    load_b.start()
-    pl.semaphore_wait(barrier, 3)
+
+    def tell(semaphore, dev):
+        pl.semaphore_signal(semaphore, inc=1, device_id=dev, device_id_type=MESH)
+
+    pl.when(col == 0)(lambda: tell(barrier, x_nbr))
+    pl.when(dep == 0)(lambda: tell(barrier, y_nbr))
+    pl.when(row == 1)(lambda: tell(barrier, sib))
+    heard = col + dep + (1 - row)
+    pl.when(heard > 0)(lambda: pl.semaphore_wait(barrier, heard))
+    pl.when(col == 1)(lambda: tell(ready.at[0], x_nbr))
+    pl.when(dep == 1)(lambda: tell(ready.at[1], y_nbr))
+    pl.when(row == 0)(lambda: tell(ready.at[2], sib))
 
     def a_copy(step):
         slot, start, size = A_STEPS[step]
@@ -80,32 +86,46 @@
     give = pltpu.make_async_remote_copy(b_ref, b4.at[2 * pair], ds, dr, device_id=sib, device_id_type=MESH)
     take = pltpu.make_async_remote_copy(b_ref, b4.at[2 * other], ds, dr, device_id=sib, device_id_type=MESH)
 
+    def send_b():
+        for step in range(STEPS):
+            b_copy(step).start()
+
+    pl.when(dep == 1)(send_b)
+    pl.when(col == 0)(lambda: pl.semaphore_wait(ready.at[0], 1))
     for step in range(STEPS):
         a_copy(step).start()
-        b_copy(step).start()
-        if step == 0:
-            give.start()
-
-    def multiply(a_view, b_view, fresh=False):
+
+    @pl.when(dep == 0)
+    def _():
+        pl.semaphore_wait(ready.at[1], 1)
+        send_b()
+
+    pl.when(row == 1)(lambda: pl.semaphore_wait(ready.at[2], 1))
+    for copy in load_a:
+        copy.start()
+    load_b.start()
+    give.start()
+
+    def multiply(pairs, fresh=False):
         @pl.loop(0, (ROWS // TM) * (COLS // TN))
         def _(t):
             rows = pl.ds(pl.multiple_of((t // (COLS // TN)) * TM, TM), TM)
             cols = pl.ds(pl.multiple_of((t % (COLS // TN)) * TN, TN), TN)
-            part = jnp.dot(a_view(rows), b_view(cols), preferred_element_type=F32)
+            part = sum(jnp.dot(a_view(rows), b_view(cols), preferred_element_type=F32) for a_view, b_view in pairs)
             if fresh:
                 acc[rows, cols] = part
             else:
                 acc[rows, cols] += part
 
-    def slot_product(slot, start, size, fresh=False):
-        multiply(lambda r: a4[slot, r, pl.ds(start, size)], lambda c: b4[slot, pl.ds(start, size), c], fresh)
+    def slot_pair(slot, start, size):
+        return lambda r: a4[slot, r, pl.ds(start, size)], lambda c: b4[slot, pl.ds(start, size), c]
 
     for copy in load_a:
         copy.wait()
     load_b.wait()
     give.wait_send()
     take.wait_recv()
-    slot_product(0, 0, Q, fresh=True)
+    multiply([slot_pair(0, 0, Q)], fresh=True)
     blast[pl.ds(0, 128), :] = b4[2, pl.ds(Q - 128, 128), :]
 
     for step in range(STEPS):
@@ -113,23 +133,25 @@
         forward(step).start()
         a_copy(step).wait_recv()
         if step == 1:
-            low = lax.broadcasted_iota(jnp.int32, (TM, 128), 1) < 64
-
-            @pl.loop(0, ROWS // TM)
+            low = lax.broadcasted_iota(jnp.int32, (256, 128), 1) < 64
+
+            @pl.loop(0, ROWS // 256)
             def _(t):
-                rows = pl.ds(pl.multiple_of(t * TM, TM), TM)
+                rows = pl.ds(pl.multiple_of(t * 256, 256), 256)
                 a1, a3 = a4[1, rows, pl.ds(Q - 128, 128)], a4[3, rows, pl.ds(Q - 128, 128)]
                 apen[rows, :] = jnp.where(low, a3, a1)
                 alast[rows, pl.ds(128, 128)] = jnp.where(low, a1, a3)
         slot, start, size = A_STEPS[step]
+        forwarded(step).wait_recv()
+        pairs = []
+        if step < LAST - 1:
+            pairs = [slot_pair(1, B_STEPS[step][0], B_STEPS[step][2]), slot_pair(3, B_STEPS[step][1], B_STEPS[step][2])]
+        elif step == LAST - 1:
+            pairs = [(lambda r: apen[r, :], lambda c: bpen[:, c])]
         if slot == 2 and step != LAST:
-            slot_product(2, start, size)
-        forwarded(step).wait_recv()
-        if step < LAST - 1:
-            slot_product(1, B_STEPS[step][0], B_STEPS[step][2])
-            slot_product(3, B_STEPS[step][1], B_STEPS[step][2])
-        elif step == LAST - 1:
-            multiply(lambda r: apen[r, :], lambda c: bpen[:, c])
+            pairs.append(slot_pair(2, start, size))
+        if pairs:
+            multiply(pairs)
 
     for step in range(STEPS):
         a_copy(step).wait_send()
@@ -172,6 +194,7 @@
                 pltpu.VMEM((4, Q, COLS), BF16),
                 pltpu.VMEM((ROWS, 128), BF16),
                 pltpu.VMEM((128, COLS), BF16),
+                pltpu.SemaphoreType.REGULAR((3,)),
                 dma((2,)), dma, dma((STEPS,)), dma((STEPS,)), dma((STEPS,)), dma((2, STEPS)), dma((STEPS,)), dma, dma,
             ],
             compiler_params=pltpu.CompilerParams(

time: 108 us -> 98 us (0.907)
  Pallas kernels: 108 us -> 97.9 us
    pallas_call x1, Pallas kernels: 106 us -> 95.5 us  [local_product(): pl.pallas_call(exchange_kernel, out_shape=(pltpu.VMEM((ROWS, COLS), F32),...]
where the time goes in v2:
time: 98 us; the launch traced here: 97.9 us
  Pallas kernels  97.9 us (100%)
    pallas_call x1, Pallas kernels, local_product(): pl.pallas_call(exchange_kernel, out_shape=(pltpu.VMEM((ROWS, COLS), F32),...  95.5 us
    pallas_call x1, Pallas kernels, local_product(): pl.pallas_call(finish_kernel, out_shape=pltpu.HBM((ROWS, COLS), BF16), in...  2.39 us

profile of v2, /device:TPU:0, one launch (start us, length us, event | category | flops | bytes accessed | tf_op | source)
XLA Modules:
  0.0 97.9 jit_solution(14159932971542592429)
XLA Ops:
  0.0 95.5 %exchange.1 = (f32[1024,2048]{1,0:T(8,128)S(1)}, bf16[1024,256]{1,0:T(8,128)(2,1)S(1)}, bf16[256,2048]{1,0:T(8,128)(2,1)S(1)}) custom-call(bf16[1024,2048]{1,0:T(8,128)(2,1)} %a_ref.1, bf16[1024,2048]{1,0:T(8,128)(2,1)} %b_ref.1), custom_call_target="tpu_custom_call" | custom-call | tf_op jit(solution)/shard_map/exchange/pallas_call | solution.py:183
  95.5 2.4 %finish.1 = bf16[1024,2048]{1,0:T(8,128)(2,1)} custom-call(f32[1024,2048]{1,0:T(8,128)S(1)} %get-tuple-element.8.acc, bf16[1024,256]{1,0:T(8,128)(2,1)S(1)} %get-tuple-element.9.alast, bf16[256,2048]{1,0:T(8,128)(2,1)S(1)} %get-tuple-element.10.blast), custom_call_target="tpu_custom_call" | custom-call | tf_op jit(solution)/shard_map/finish/pallas_call | solution.py:204

commit v3 on v2

v3 whole, which is shorter than its diff:
```python
import jax
import jax.numpy as jnp
from jax import lax
from jax.experimental import pallas as pl
from jax.experimental.pallas import tpu as pltpu
from jax.sharding import PartitionSpec as P

MESH = pl.DeviceIdType.MESH
BF16, F32 = jnp.bfloat16, jnp.float32

Q = 1024
ROWS, COLS = 1024, 2048

B_STEPS = [(0, 0, 512), (512, 512, 256), (768, 768, 128), (960, 896, 64), (896, 960, 64)]
A_STEPS = [(3, 0, 1024), (2, 0, 512), (2, 512, 256), (2, 768, 128), (2, 896, 128)]
LAST = len(B_STEPS) - 1
PEN = LAST - 1
EARLY = PEN
HALF = B_STEPS[LAST][2] // 2
TM, TN = 512, 1024


def exchange_kernel(a_ref, b_ref, acc, alast, blast, a4, b4, apen, bpen, relay_out, relay_in,
                    ready, loaded, sent, xr, yr, dr, rr):
    dep, col, row = lax.axis_index("depth"), lax.axis_index("col"), lax.axis_index("row")
    x_nbr, y_nbr, sib = (dep, 1 - col, row), (1 - dep, col, row), (dep, col, 1 - row)
    pair = (row + col) % 2
    other = 1 - pair
    near = pl.multiple_of(dep * Q, Q)
    far = pl.multiple_of((1 - dep) * Q, Q)
    main, more = sent.at[0], sent.at[1]

    def remote(src, dst, send_sem, recv_sem, dev):
        return pltpu.make_async_remote_copy(src, dst, send_sem, recv_sem, device_id=dev, device_id_type=MESH)

    barrier = pltpu.get_barrier_semaphore()

    def tell(semaphore, dev):
        pl.semaphore_signal(semaphore, inc=1, device_id=dev, device_id_type=MESH)

    pl.when(col == 0)(lambda: tell(barrier, x_nbr))
    pl.when(dep == 0)(lambda: tell(barrier, y_nbr))
    pl.when(row == 1)(lambda: tell(barrier, sib))
    heard = col + dep + (1 - row)
    pl.when(heard > 0)(lambda: pl.semaphore_wait(barrier, heard))
    pl.when(col == 1)(lambda: tell(ready.at[0], x_nbr))
    pl.when(dep == 1)(lambda: tell(ready.at[1], y_nbr))
    pl.when(row == 0)(lambda: tell(ready.at[2], sib))

    def a_copy(step, rows=ROWS):
        slot, start, size = A_STEPS[step]
        src = a_ref.at[pl.ds(0, rows), pl.ds(pl.multiple_of((near if slot == 2 else far) + start, 128), size)]
        dst = alast.at[pl.ds(0, rows), pl.ds(0, 128)] if step == LAST else a4.at[slot, :, pl.ds(start, size)]
        return remote(src, dst, main, xr.at[step], x_nbr)

    def b_start(step, which):
        s1, s3, _ = B_STEPS[step]
        return s1 + which * (s3 - s1)

    def b_place(step, which):
        if step == PEN:
            return bpen.at[pl.ds(pl.multiple_of((1 - which) * 64, 64), 64)]
        return b4.at[2 * which + 1, pl.ds(B_STEPS[step][0], B_STEPS[step][2])]

    def b_copy(step):
        src = b_ref.at[pl.ds(pl.multiple_of(b_start(step, pair), 64), B_STEPS[step][2])]
        return remote(src, b_place(step, pair), main, yr.at[pair, step], y_nbr)

    def forward(step, which):
        return remote(b_place(step, which), b_place(step, which), main, yr.at[which, step], sib)

    def tail_place(which, half):
        return blast.at[pl.ds(pl.multiple_of(128 + which * 64 + half * HALF, HALF), HALF)]

    def tail_copy(half):
        src = b_ref.at[pl.ds(pl.multiple_of(b_start(LAST, pair) + half * HALF, HALF), HALF)]
        return remote(src, tail_place(pair, half), main, yr.at[pair, LAST + half], y_nbr)

    def tail_forward(which, half, sem=main):
        return remote(tail_place(which, half), tail_place(which, half), sem, yr.at[which, LAST + half], sib)

    extra = remote(
        b4.at[2 * other, pl.ds(pl.multiple_of(b_start(LAST, other) + HALF, HALF), HALF)], tail_place(other, 1),
        more, yr.at[other, LAST + 1], y_nbr)
    relay_rows = pl.ds(ROWS // 2, ROWS // 2)
    relay_cols = pl.ds(pl.multiple_of(near + A_STEPS[LAST][1], 128), 128)
    relay_give = remote(a_ref.at[relay_rows, relay_cols], relay_out, main, rr.at[0], sib)
    relay_send = remote(relay_out, relay_in, more, rr.at[1], x_nbr)
    relay_end = remote(relay_in, alast.at[relay_rows, pl.ds(0, 128)], more, rr.at[0], sib)

    give = remote(b_ref, b4.at[2 * pair], main, dr, sib)
    take = remote(b_ref, b4.at[2 * other], main, dr, sib)

    def send_b():
        for step in range(EARLY):
            b_copy(step).start()

    pl.when(dep == 1)(send_b)
    pl.when(col == 0)(lambda: pl.semaphore_wait(ready.at[0], 1))
    for step in range(EARLY):
        a_copy(step).start()

    @pl.when(dep == 0)
    def _():
        pl.semaphore_wait(ready.at[1], 1)
        send_b()

    pl.when(row == 1)(lambda: pl.semaphore_wait(ready.at[2], 1))
    pltpu.make_async_copy(a_ref.at[:, pl.ds(near, Q)], a4.at[0], loaded).start()
    pltpu.make_async_copy(a_ref.at[:, pl.ds(far, Q)], a4.at[1], loaded).start()
    pltpu.make_async_copy(b_ref, b4.at[2 * pair], loaded).start()

    @pl.when(row == 0)
    def _():
        relay_give.start()
        a_copy(PEN).start()
        b_copy(PEN).start()
        a_copy(LAST, ROWS // 2).start()
        tail_copy(0).start()

    give.start()

    @pl.when(row == 1)
    def _():
        relay_give.wait_recv()
        relay_send.start()
        a_copy(PEN).start()
        a_copy(LAST).start()

    pltpu.make_async_copy(b4.at[pl.ds(0, 2)], b4.at[pl.ds(0, 2)], loaded).wait()
    take.wait_recv()

    @pl.when(row == 1)
    def _():
        extra.start()
        b_copy(PEN).start()
        tail_copy(0).start()
        tail_copy(1).start()

    def multiply(a_view, b_view, fresh=False):
        @pl.loop(0, (ROWS // TM) * (COLS // TN))
        def _(t):
            rows = pl.ds(pl.multiple_of((t // (COLS // TN)) * TM, TM), TM)
            cols = pl.ds(pl.multiple_of((t % (COLS // TN)) * TN, TN), TN)
            part = jnp.dot(a_view(rows), b_view(cols), preferred_element_type=F32)
            if fresh:
                acc[rows, cols] = part
            else:
                acc[rows, cols] += part

    multiply(lambda r: a4[0, r, :], lambda c: b4[0, :, c], fresh=True)
    blast[pl.ds(0, 128), :] = b4[2, pl.ds(Q - 128, 128), :]

    for step in range(PEN):
        b_copy(step).wait_recv()
        forward(step, pair).start()
        a_copy(step).wait_recv()
        if step == 0:
            low = lax.broadcasted_iota(jnp.int32, (256, 128), 1) < 64

            @pl.loop(0, ROWS // 256)
            def _(t):
                rows = pl.ds(pl.multiple_of(t * 256, 256), 256)
                a1, a3 = a4[1, rows, pl.ds(Q - 128, 128)], a4[3, rows, pl.ds(Q - 128, 128)]
                apen[rows, :] = jnp.where(low, a3, a1)
                alast[rows, pl.ds(128, 128)] = jnp.where(low, a1, a3)

        forward(step, other).wait_recv()
        parts = [(slot, pl.ds(B_STEPS[step][0], B_STEPS[step][2])) for slot in (1, 3)]
        slot, start, size = A_STEPS[step]
        if slot == 2:
            parts.append((2, pl.ds(start, size)))
        multiply(lambda r: jnp.concatenate([a4[s, r, k] for s, k in parts], axis=1),
                 lambda c: jnp.concatenate([b4[s, k, c] for s, k in parts], axis=0))

    @pl.when(row == 1)
    def _():
        relay_send.wait_recv()
        relay_end.start()
        extra.wait_recv()
        tail_forward(other, 1, more).start()

    b_copy(PEN).wait_recv()
    forward(PEN, pair).start()
    a_copy(PEN).wait_recv()

    @pl.when(row == 0)
    def _():
        tail_copy(0).wait_recv()
        tail_forward(pair, 0).start()

    forward(PEN, other).wait_recv()
    pen_cols = pl.ds(A_STEPS[PEN][1], 128)
    multiply(lambda r: jnp.concatenate([apen[r, :], a4[2, r, pen_cols]], axis=1),
             lambda c: jnp.concatenate([bpen[:, c], b4[2, pen_cols, c]], axis=0))

    @pl.when(row == 0)
    def _():
        a_copy(LAST, ROWS // 2).wait_recv()
        relay_end.wait_recv()
        tail_forward(pair, 1).wait_recv()
        tail_forward(other, 0).wait_recv()
        tail_forward(other, 1).wait_recv()
        every = b4.at[:, pl.ds(0, Q - Q // 64)]
        pltpu.make_async_copy(every, every, main).wait()

    @pl.when(row == 1)
    def _():
        for half in range(2):
            tail_copy(half).wait_recv()
            tail_forward(pair, half).start()
        a_copy(LAST).wait_recv()
        tail_forward(other, 0).wait_recv()
        pltpu.make_async_copy(b4, b4, main).wait()
        pltpu.make_async_copy(bpen, bpen, more).wait()


def finish_kernel(acc, alast, blast, c_ref, stage, done):
    blk = 128
    for t in range(ROWS // blk):
        rows = pl.ds(t * blk, blk)
        tail = jnp.dot(alast[rows, :], blast[...], preferred_element_type=F32)
        stage[rows, :] = (acc[rows, :] + tail).astype(BF16)
        pltpu.make_async_copy(stage.at[rows], c_ref.at[rows], done).start()
    pltpu.make_async_copy(stage, c_ref, done).wait()


def solution(mesh):
    hbm = pl.BlockSpec(memory_space=pltpu.HBM)
    vmem = pl.BlockSpec(memory_space=pltpu.VMEM)
    dma = pltpu.SemaphoreType.DMA

    def local_product(a_blk, b_blk):
        a_blk = pltpu.with_memory_space_constraint(a_blk, pltpu.HBM)
        b_blk = pltpu.with_memory_space_constraint(b_blk, pltpu.HBM)
        acc, alast, blast = pl.pallas_call(
            exchange_kernel,
            out_shape=(
                pltpu.VMEM((ROWS, COLS), F32),
                pltpu.VMEM((ROWS, 256), BF16),
                pltpu.VMEM((256, COLS), BF16),
            ),
            in_specs=[hbm, hbm],
            out_specs=(vmem, vmem, vmem),
            scratch_shapes=[
                pltpu.VMEM((4, ROWS, Q), BF16),
                pltpu.VMEM((4, Q, COLS), BF16),
                pltpu.VMEM((ROWS, 128), BF16),
                pltpu.VMEM((128, COLS), BF16),
                pltpu.VMEM((ROWS // 2, 128), BF16),
                pltpu.VMEM((ROWS // 2, 128), BF16),
                pltpu.SemaphoreType.REGULAR((3,)),
                dma, dma((2,)), dma((LAST + 1,)), dma((2, LAST + 2)), dma, dma((2,)),
            ],
            compiler_params=pltpu.CompilerParams(
                collective_id=0, has_side_effects=True, vmem_limit_bytes=44 * 2**20),
            name="exchange",
        )(a_blk, b_blk)
        return pl.pallas_call(
            finish_kernel,
            out_shape=pltpu.HBM((ROWS, COLS), BF16),
            in_specs=[vmem, vmem, vmem],
            out_specs=hbm,
            scratch_shapes=[pltpu.VMEM((ROWS, COLS), BF16), dma],
            compiler_params=pltpu.CompilerParams(vmem_limit_bytes=24 * 2**20),
            name="finish",
        )(acc, alast, blast)

    spec = P(("row", "depth"), "col")
    return jax.shard_map(local_product, mesh=mesh, in_specs=(spec, spec), out_specs=spec, check_vma=False)
```

time: 98 us -> 97.2 us (level)
  no operation moved by 1% of the time
where the time goes in v3:
time: 97.2 us
  Pallas kernels  97.2 us (100%)
    pallas_call x1, Pallas kernels, local_product(): pl.pallas_call(exchange_kernel, out_shape=(pltpu.VMEM((ROWS, COLS), F32),...  94.8 us
    pallas_call x1, Pallas kernels, local_product(): pl.pallas_call(finish_kernel, out_shape=pltpu.HBM((ROWS, COLS), BF16), in...  2.32 us

profile of v3, /device:TPU:0, one launch (start us, length us, event | category | flops | bytes accessed | tf_op | source)
XLA Modules:
  0.0 97.2 jit_solution(12411816226490240467)
XLA Ops:
  0.0 94.8 %exchange.1 = (f32[1024,2048]{1,0:T(8,128)S(1)}, bf16[1024,256]{1,0:T(8,128)(2,1)S(1)}, bf16[256,2048]{1,0:T(8,128)(2,1)S(1)}) custom-call(bf16[1024,2048]{1,0:T(8,128)(2,1)} %a_ref.1, bf16[1024,2048]{1,0:T(8,128)(2,1)} %b_ref.1), custom_call_target="tpu_custom_call" | custom-call | tf_op jit(solution)/shard_map/exchange/pallas_call | solution.py:236
  94.8 2.3 %finish.1 = bf16[1024,2048]{1,0:T(8,128)(2,1)} custom-call(f32[1024,2048]{1,0:T(8,128)S(1)} %get-tuple-element.8.acc, bf16[1024,256]{1,0:T(8,128)(2,1)S(1)} %get-tuple-element.9.alast, bf16[256,2048]{1,0:T(8,128)(2,1)S(1)} %get-tuple-element.10.blast), custom_call_target="tpu_custom_call" | custom-call | tf_op jit(solution)/shard_map/finish/pallas_call | solution.py:259

commit v4 on v3

v4 whole, which is shorter than its diff:
```python
import jax
import jax.numpy as jnp
from jax import lax
from jax.experimental import pallas as pl
from jax.experimental.pallas import tpu as pltpu
from jax.sharding import PartitionSpec as P

MESH = pl.DeviceIdType.MESH
BF16, F32 = jnp.bfloat16, jnp.float32

Q = 1024
ROWS, COLS = 1024, 2048

B_STEPS = [(0, 512, 0, COLS), (512, 256, 0, COLS), (768, 128, 0, COLS), (896, 128, 0, 1024), (896, 128, 1024, 768),
           (896, 128, 1792, 256)]
A_STEPS = [(3, 0, ROWS), (2, 0, 512), (2, 512, 256), (2, 768, 128), (2, 896, 128)]
EARLY = 3
PEN, TAIL, END = 3, 4, 5
LAST = 4
LEFT = 1024
KEEP = 64
TN = 1024


def exchange_kernel(a_ref, b_ref, acc, left, alast, blast, a4, b4, relay_out, relay_in,
                    ready, loaded, sent, xr, yr, dr, rr):
    dep, col, row = lax.axis_index("depth"), lax.axis_index("col"), lax.axis_index("row")
    x_nbr, y_nbr, sib = (dep, 1 - col, row), (1 - dep, col, row), (dep, col, 1 - row)
    pair = (row + col) % 2
    other = 1 - pair
    near = pl.multiple_of(dep * Q, Q)
    far = pl.multiple_of((1 - dep) * Q, Q)
    main, more = sent.at[0], sent.at[1]

    def remote(src, dst, send_sem, recv_sem, dev):
        return pltpu.make_async_remote_copy(src, dst, send_sem, recv_sem, device_id=dev, device_id_type=MESH)

    barrier = pltpu.get_barrier_semaphore()

    def tell(semaphore, dev):
        pl.semaphore_signal(semaphore, inc=1, device_id=dev, device_id_type=MESH)

    pl.when(col == 0)(lambda: tell(barrier, x_nbr))
    pl.when(dep == 0)(lambda: tell(barrier, y_nbr))
    pl.when(row == 1)(lambda: tell(barrier, sib))
    heard = col + dep + (1 - row)
    pl.when(heard > 0)(lambda: pl.semaphore_wait(barrier, heard))
    pl.when(col == 1)(lambda: tell(ready.at[0], x_nbr))
    pl.when(dep == 1)(lambda: tell(ready.at[1], y_nbr))
    pl.when(row == 0)(lambda: tell(ready.at[2], sib))

    def a_copy(step, keep=None):
        slot, first, rows = A_STEPS[step]
        rows = pl.ds(first, keep or rows)
        src = a_ref.at[rows, pl.ds(near if slot == 2 else far, Q)]
        return remote(src, a4.at[slot, rows], main, xr.at[step], x_nbr)

    def b_place(step, which):
        r, rows, c, cols = B_STEPS[step]
        if step >= TAIL:
            return blast.at[pl.ds(pl.multiple_of(which * rows, rows), rows), pl.ds(c - LEFT, cols)]
        return b4.at[2 * which + 1, pl.ds(r, rows), pl.ds(c, cols)]

    def b_copy(step):
        r, rows, c, cols = B_STEPS[step]
        return remote(b_ref.at[pl.ds(r, rows), pl.ds(c, cols)], b_place(step, pair), main, yr.at[pair, step], y_nbr)

    def forward(step, which, sem=main):
        return remote(b_place(step, which), b_place(step, which), sem, yr.at[which, step], sib)

    end_rows, end_cols = pl.ds(B_STEPS[END][0], B_STEPS[END][1]), pl.ds(B_STEPS[END][2], B_STEPS[END][3])
    extra = remote(b4.at[2 * other, end_rows, end_cols], b_place(END, other), more, yr.at[other, END], y_nbr)
    relay_rows = pl.ds(A_STEPS[LAST][1] + KEEP, A_STEPS[LAST][2] - KEEP)
    relay_give = remote(a_ref.at[relay_rows, pl.ds(near, Q)], relay_out, more, rr.at[0], sib)
    relay_send = remote(relay_out, relay_in, more, rr.at[1], x_nbr)
    relay_end = remote(relay_in, a4.at[2, relay_rows], more, rr.at[0], sib)

    give = remote(b_ref, b4.at[2 * pair], main, dr, sib)
    take = remote(b_ref, b4.at[2 * other], main, dr, sib)

    def send_b():
        for step in range(EARLY):
            b_copy(step).start()

    pl.when(dep == 1)(send_b)
    pl.when(col == 0)(lambda: pl.semaphore_wait(ready.at[0], 1))
    for step in range(EARLY):
        a_copy(step).start()

    @pl.when(dep == 0)
    def _():
        pl.semaphore_wait(ready.at[1], 1)
        send_b()

    pl.when(row == 1)(lambda: pl.semaphore_wait(ready.at[2], 1))
    pltpu.make_async_copy(a_ref.at[:, pl.ds(near, Q)], a4.at[0], loaded).start()
    pltpu.make_async_copy(a_ref.at[:, pl.ds(far, Q)], a4.at[1], loaded).start()
    pltpu.make_async_copy(b_ref, b4.at[2 * pair], loaded).start()

    @pl.when(row == 0)
    def _():
        relay_give.start()
        a_copy(PEN).start()
        a_copy(LAST, KEEP).start()
        b_copy(PEN).start()
        b_copy(TAIL).start()

    give.start()

    @pl.when(row == 1)
    def _():
        relay_give.wait_recv()
        relay_send.start()
        a_copy(PEN).start()
        a_copy(LAST).start()

    pltpu.make_async_copy(b4.at[pl.ds(0, 2)], b4.at[pl.ds(0, 2)], loaded).wait()
    take.wait_recv()

    @pl.when(row == 1)
    def _():
        extra.start()
        for step in (PEN, TAIL, END):
            b_copy(step).start()

    def multiply(parts, first=0, count=ROWS, tm=512, columns=(0, COLS), fresh=False, out=acc):
        across = (columns[1] - columns[0]) // TN

        @pl.loop(0, (count // tm) * across)
        def _(t):
            rows = pl.ds(pl.multiple_of(first + (t // across) * tm, 64), tm)
            cols = pl.ds(pl.multiple_of(columns[0] + (t % across) * TN, TN), TN)
            lhs = jnp.concatenate([a4[s, rows, k] for s, k in parts], axis=1)
            rhs = jnp.concatenate([b4[s, k, cols] for s, k in parts], axis=0)
            part = jnp.dot(lhs, rhs, preferred_element_type=F32)
            out[rows, cols] = (part if fresh else acc[rows, cols] + part).astype(out.dtype)

    whole = pl.ds(0, Q)
    multiply([(0, whole)], fresh=True)

    for step in range(EARLY):
        b_copy(step).wait_recv()
        forward(step, pair).start()
        a_copy(step).wait_recv()
        forward(step, other).wait_recv()
        k = pl.ds(B_STEPS[step][0], B_STEPS[step][1])
        multiply([(1, k), (3, k)])
        slot, first, rows = A_STEPS[step]
        if slot == 2:
            multiply([(2, whole)], first, rows, tm=256)

    ends = pl.ds(B_STEPS[PEN][0], B_STEPS[PEN][1])
    alast[:, pl.ds(0, 128)] = a4[1, :, ends]
    alast[:, pl.ds(128, 128)] = a4[3, :, ends]

    @pl.when(row == 1)
    def _():
        relay_send.wait_recv()
        relay_end.start()
        extra.wait_recv()
        forward(END, other, more).start()

    done_rows = A_STEPS[LAST][1]
    b_copy(PEN).wait_recv()
    forward(PEN, pair).start()
    a_copy(PEN).wait_recv()
    multiply([(2, whole)], A_STEPS[PEN][1], A_STEPS[PEN][2], tm=128)
    forward(PEN, other).wait_recv()
    multiply([(1, ends), (3, ends)], 0, done_rows, tm=448, columns=(0, LEFT), out=left)
    multiply([(1, ends), (3, ends)], done_rows, ROWS - done_rows, tm=128, columns=(0, LEFT))

    def last_rows():
        multiply([(2, whole)], done_rows, ROWS - done_rows, tm=128, columns=(LEFT, COLS))
        multiply([(2, whole)], done_rows, ROWS - done_rows, tm=128, columns=(0, LEFT), out=left)

    @pl.when(row == 0)
    def _():
        a_copy(LAST, KEEP).wait_recv()
        relay_end.wait_recv()

    @pl.when(row == 1)
    def _():
        b_copy(TAIL).wait_recv()
        forward(TAIL, pair).start()
        b_copy(END).wait_recv()
        forward(END, pair).start()
        a_copy(LAST).wait_recv()

    last_rows()

    @pl.when(row == 0)
    def _():
        b_copy(TAIL).wait_recv()
        forward(TAIL, pair).start()

    forward(TAIL, other).wait_recv()

    @pl.when(row == 0)
    def _():
        forward(END, pair).wait_recv()
        forward(END, other).wait_recv()
        every = b4.at[:, pl.ds(0, Q - Q // 64)]
        pltpu.make_async_copy(every, every, main).wait()
        pltpu.make_async_copy(relay_out, relay_out, more).wait()

    @pl.when(row == 1)
    def _():
        pltpu.make_async_copy(b4, b4, main).wait()
        rest = alast.at[pl.ds(0, 768)]
        pltpu.make_async_copy(rest, rest, more).wait()


def finish_kernel(acc, left, alast, blast, c_ref, stage, done):
    pltpu.make_async_copy(left, c_ref.at[:, pl.ds(0, LEFT)], done).start()
    blk = 256
    right = pl.ds(LEFT, COLS - LEFT)
    for t in range(ROWS // blk):
        rows = pl.ds(t * blk, blk)
        tail = jnp.dot(alast[rows, :], blast[...], preferred_element_type=F32)
        stage[rows, :] = (acc[rows, right] + tail).astype(BF16)
        pltpu.make_async_copy(stage.at[rows], c_ref.at[rows, right], done).start()
    pltpu.make_async_copy(c_ref, c_ref, done).wait()


def solution(mesh):
    hbm = pl.BlockSpec(memory_space=pltpu.HBM)
    vmem = pl.BlockSpec(memory_space=pltpu.VMEM)
    dma = pltpu.SemaphoreType.DMA

    def local_product(a_blk, b_blk):
        a_blk = pltpu.with_memory_space_constraint(a_blk, pltpu.HBM)
        b_blk = pltpu.with_memory_space_constraint(b_blk, pltpu.HBM)
        partial = pl.pallas_call(
            exchange_kernel,
            out_shape=(
                pltpu.VMEM((ROWS, COLS), F32),
                pltpu.VMEM((ROWS, LEFT), BF16),
                pltpu.VMEM((ROWS, 256), BF16),
                pltpu.VMEM((256, COLS - LEFT), BF16),
            ),
            in_specs=[hbm, hbm],
            out_specs=(vmem,) * 4,
            scratch_shapes=[
                pltpu.VMEM((4, ROWS, Q), BF16),
                pltpu.VMEM((4, Q, COLS), BF16),
                pltpu.VMEM((64, Q), BF16),
                pltpu.VMEM((64, Q), BF16),
                pltpu.SemaphoreType.REGULAR((3,)),
                dma, dma((2,)), dma((LAST + 1,)), dma((2, END + 1)), dma, dma((2,)),
            ],
            compiler_params=pltpu.CompilerParams(
                collective_id=0, has_side_effects=True, vmem_limit_bytes=44 * 2**20),
            name="exchange",
        )(a_blk, b_blk)
        return pl.pallas_call(
            finish_kernel,
            out_shape=pltpu.HBM((ROWS, COLS), BF16),
            in_specs=[vmem] * 4,
            out_specs=hbm,
            scratch_shapes=[pltpu.VMEM((ROWS, COLS - LEFT), BF16), dma],
            compiler_params=pltpu.CompilerParams(vmem_limit_bytes=24 * 2**20),
            name="finish",
        )(*partial)

    spec = P(("row", "depth"), "col")
    return jax.shard_map(local_product, mesh=mesh, in_specs=(spec, spec), out_specs=spec, check_vma=False)
```

time: 97.2 us -> 96.9 us (level)
  no operation moved by 1% of the time
where the time goes in v4:
time: 96.9 us; the launch traced here: 96.8 us
  Pallas kernels  96.8 us (100%)
    pallas_call x1, Pallas kernels, local_product(): pl.pallas_call(exchange_kernel, out_shape=(pltpu.VMEM((ROWS, COLS), F32),...  94.7 us
    pallas_call x1, Pallas kernels, local_product(): pl.pallas_call(finish_kernel, out_shape=pltpu.HBM((ROWS, COLS), BF16), in...  2.03 us

profile of v4, /device:TPU:0, one launch (start us, length us, event | category | flops | bytes accessed | tf_op | source)
XLA Modules:
  0.0 96.8 jit_solution(14470932010560274375)
XLA Ops:
  0.0 94.7 %exchange.1 = (f32[1024,2048]{1,0:T(8,128)S(1)}, bf16[1024,1024]{1,0:T(8,128)(2,1)S(1)}, bf16[1024,256]{1,0:T(8,128)(2,1)S(1)}, bf16[256,1024]{1,0:T(8,128)(2,1)S(1)}) custom-call(bf16[1024,2048]{1,0:T(8,128)(2,1)} %a_ref.1, bf16[1024,2048]{1,0:T(8,128)(2,1)} %b_ref.1), custom_call_target="tpu_custom_call" | custom-call | tf_op jit(solution)/shard_map/exchange/pallas_call | solution.py:233
  94.7 2.0 %finish.1 = bf16[1024,2048]{1,0:T(8,128)(2,1)} custom-call(f32[1024,2048]{1,0:T(8,128)S(1)} %get-tuple-element.9.acc, bf16[1024,1024]{1,0:T(8,128)(2,1)S(1)} %get-tuple-element.10.left, bf16[1024,256]{1,0:T(8,128)(2,1)S(1)} %get-tuple-element.11.alast, bf16[256,1024]{1,0:T(8,128)(2,1)S(1)} %get-tuple-element.12.blast), custom_call_target="tpu_custom_call" | custom-call | tf_op jit(solution)/shard_map/finish/pallas_call | solution.py:255

commit v5 on v4

--- a/solution.py
+++ b/solution.py
@@ -23,7 +23,7 @@
 
 
 def exchange_kernel(a_ref, b_ref, acc, left, alast, blast, a4, b4, relay_out, relay_in,
-                    ready, loaded, sent, xr, yr, dr, rr):
+                    ready, loaded, sent, last, yr, direct, fin, relayed):
     dep, col, row = lax.axis_index("depth"), lax.axis_index("col"), lax.axis_index("row")
     x_nbr, y_nbr, sib = (dep, 1 - col, row), (1 - dep, col, row), (dep, col, 1 - row)
     pair = (row + col) % 2
@@ -53,7 +53,7 @@
         slot, first, rows = A_STEPS[step]
         rows = pl.ds(first, keep or rows)
         src = a_ref.at[rows, pl.ds(near if slot == 2 else far, Q)]
-        return remote(src, a4.at[slot, rows], main, xr.at[step], x_nbr)
+        return remote(src, a4.at[slot, rows], main, last if step == LAST else yr.at[other, step], x_nbr)
 
     def b_place(step, which):
         r, rows, c, cols = B_STEPS[step]
@@ -63,20 +63,30 @@
 
     def b_copy(step):
         r, rows, c, cols = B_STEPS[step]
-        return remote(b_ref.at[pl.ds(r, rows), pl.ds(c, cols)], b_place(step, pair), main, yr.at[pair, step], y_nbr)
+        return remote(b_ref.at[pl.ds(r, rows), pl.ds(c, cols)], b_place(step, pair), main,
+                      direct.at[step - TAIL] if step >= TAIL else yr.at[pair, step], y_nbr)
 
     def forward(step, which, sem=main):
-        return remote(b_place(step, which), b_place(step, which), sem, yr.at[which, step], sib)
+        return remote(b_place(step, which), b_place(step, which), sem, fin if step >= TAIL else yr.at[which, step], sib)
 
     end_rows, end_cols = pl.ds(B_STEPS[END][0], B_STEPS[END][1]), pl.ds(B_STEPS[END][2], B_STEPS[END][3])
-    extra = remote(b4.at[2 * other, end_rows, end_cols], b_place(END, other), more, yr.at[other, END], y_nbr)
+    extra = remote(b4.at[2 * other, end_rows, end_cols], b_place(END, other), more, direct.at[2], y_nbr)
     relay_rows = pl.ds(A_STEPS[LAST][1] + KEEP, A_STEPS[LAST][2] - KEEP)
-    relay_give = remote(a_ref.at[relay_rows, pl.ds(near, Q)], relay_out, more, rr.at[0], sib)
-    relay_send = remote(relay_out, relay_in, more, rr.at[1], x_nbr)
-    relay_end = remote(relay_in, a4.at[2, relay_rows], more, rr.at[0], sib)
-
-    give = remote(b_ref, b4.at[2 * pair], main, dr, sib)
-    take = remote(b_ref, b4.at[2 * other], main, dr, sib)
+    relay_give = remote(a_ref.at[relay_rows, pl.ds(near, Q)], relay_out, more, relayed, sib)
+    relay_send = remote(relay_out, relay_in, more, direct.at[2], x_nbr)
+    relay_end = remote(relay_in, a4.at[2, relay_rows], more, last, sib)
+
+    give = remote(b_ref, b4.at[2 * pair], main, loaded, sib)
+
+    def all_of(semaphore, ref):
+        pltpu.make_async_copy(ref, ref, semaphore).wait()
+
+    def pieces(*sizes):
+        return b4.at[0, pl.ds(0, sum(sizes) // COLS)]
+
+    def size(step):
+        return B_STEPS[step][1] * B_STEPS[step][3]
+
 
     def send_b():
         for step in range(EARLY):
@@ -114,8 +124,7 @@
         a_copy(PEN).start()
         a_copy(LAST).start()
 
-    pltpu.make_async_copy(b4.at[pl.ds(0, 2)], b4.at[pl.ds(0, 2)], loaded).wait()
-    take.wait_recv()
+    all_of(loaded, b4.at[pl.ds(0, 3)])
 
     @pl.when(row == 1)
     def _():
@@ -139,9 +148,8 @@
     multiply([(0, whole)], fresh=True)
 
     for step in range(EARLY):
-        b_copy(step).wait_recv()
+        all_of(yr.at[pair, step], pieces(size(step), A_STEPS[step][2] * Q))
         forward(step, pair).start()
-        a_copy(step).wait_recv()
         forward(step, other).wait_recv()
         k = pl.ds(B_STEPS[step][0], B_STEPS[step][1])
         multiply([(1, k), (3, k)])
@@ -155,15 +163,13 @@
 
     @pl.when(row == 1)
     def _():
-        relay_send.wait_recv()
+        all_of(direct.at[2], pieces(size(END), (ROWS - A_STEPS[LAST][1] - KEEP) * Q))
         relay_end.start()
-        extra.wait_recv()
         forward(END, other, more).start()
 
     done_rows = A_STEPS[LAST][1]
-    b_copy(PEN).wait_recv()
+    all_of(yr.at[pair, PEN], pieces(size(PEN), A_STEPS[PEN][2] * Q))
     forward(PEN, pair).start()
-    a_copy(PEN).wait_recv()
     multiply([(2, whole)], A_STEPS[PEN][1], A_STEPS[PEN][2], tm=128)
     forward(PEN, other).wait_recv()
     multiply([(1, ends), (3, ends)], 0, done_rows, tm=448, columns=(0, LEFT), out=left)
@@ -173,19 +179,14 @@
         multiply([(2, whole)], done_rows, ROWS - done_rows, tm=128, columns=(LEFT, COLS))
         multiply([(2, whole)], done_rows, ROWS - done_rows, tm=128, columns=(0, LEFT), out=left)
 
-    @pl.when(row == 0)
-    def _():
-        a_copy(LAST, KEEP).wait_recv()
-        relay_end.wait_recv()
-
     @pl.when(row == 1)
     def _():
         b_copy(TAIL).wait_recv()
         forward(TAIL, pair).start()
         b_copy(END).wait_recv()
         forward(END, pair).start()
-        a_copy(LAST).wait_recv()
-
+
+    a_copy(LAST).wait_recv()
     last_rows()
 
     @pl.when(row == 0)
@@ -193,26 +194,22 @@
         b_copy(TAIL).wait_recv()
         forward(TAIL, pair).start()
 
-    forward(TAIL, other).wait_recv()
-
     @pl.when(row == 0)
     def _():
-        forward(END, pair).wait_recv()
-        forward(END, other).wait_recv()
-        every = b4.at[:, pl.ds(0, Q - Q // 64)]
-        pltpu.make_async_copy(every, every, main).wait()
-        pltpu.make_async_copy(relay_out, relay_out, more).wait()
-
-    @pl.when(row == 1)
-    def _():
-        pltpu.make_async_copy(b4, b4, main).wait()
-        rest = alast.at[pl.ds(0, 768)]
-        pltpu.make_async_copy(rest, rest, more).wait()
+        all_of(fin, pieces(size(TAIL), size(END), size(END)))
+        all_of(main, b4.at[:, pl.ds(0, Q - Q // 64)])
+        all_of(more, relay_out)
+
+    @pl.when(row == 1)
+    def _():
+        all_of(fin, pieces(size(TAIL)))
+        all_of(main, b4)
+        all_of(more, alast.at[pl.ds(0, 768)])
 
 
 def finish_kernel(acc, left, alast, blast, c_ref, stage, done):
     pltpu.make_async_copy(left, c_ref.at[:, pl.ds(0, LEFT)], done).start()
-    blk = 256
+    blk = 128
     right = pl.ds(LEFT, COLS - LEFT)
     for t in range(ROWS // blk):
         rows = pl.ds(t * blk, blk)
@@ -246,7 +243,7 @@
                 pltpu.VMEM((64, Q), BF16),
                 pltpu.VMEM((64, Q), BF16),
                 pltpu.SemaphoreType.REGULAR((3,)),
-                dma, dma((2,)), dma((LAST + 1,)), dma((2, END + 1)), dma, dma((2,)),
+                dma, dma((2,)), dma, dma((2, TAIL)), dma((3,)), dma, dma,
             ],
             compiler_params=pltpu.CompilerParams(
                 collective_id=0, has_side_effects=True, vmem_limit_bytes=44 * 2**20),

time: 96.9 us -> 96.8 us (level)
  no operation moved by 1% of the time
where the time goes in v5:
time: 96.8 us; the launch traced here: 96.7 us
  Pallas kernels  96.7 us (100%)
    pallas_call x1, Pallas kernels, local_product(): pl.pallas_call(exchange_kernel, out_shape=(pltpu.VMEM((ROWS, COLS), F32),...  94.7 us
    pallas_call x1, Pallas kernels, local_product(): pl.pallas_call(finish_kernel, out_shape=pltpu.HBM((ROWS, COLS), BF16), in...  2.02 us

profile of v5, /device:TPU:0, one launch (start us, length us, event | category | flops | bytes accessed | tf_op | source)
XLA Modules:
  0.0 96.7 jit_solution(10039530047960961366)
XLA Ops:
  0.0 94.7 %exchange.1 = (f32[1024,2048]{1,0:T(8,128)S(1)}, bf16[1024,1024]{1,0:T(8,128)(2,1)S(1)}, bf16[1024,256]{1,0:T(8,128)(2,1)S(1)}, bf16[256,1024]{1,0:T(8,128)(2,1)S(1)}) custom-call(bf16[1024,2048]{1,0:T(8,128)(2,1)} %a_ref.1, bf16[1024,2048]{1,0:T(8,128)(2,1)} %b_ref.1), custom_call_target="tpu_custom_call" | custom-call | tf_op jit(solution)/shard_map/exchange/pallas_call | solution.py:230
  94.7 2.0 %finish.1 = bf16[1024,2048]{1,0:T(8,128)(2,1)} custom-call(f32[1024,2048]{1,0:T(8,128)S(1)} %get-tuple-element.9.acc, bf16[1024,1024]{1,0:T(8,128)(2,1)S(1)} %get-tuple-element.10.left, bf16[1024,256]{1,0:T(8,128)(2,1)S(1)} %get-tuple-element.11.alast, bf16[256,1024]{1,0:T(8,128)(2,1)S(1)} %get-tuple-element.12.blast), custom_call_target="tpu_custom_call" | custom-call | tf_op jit(solution)/shard_map/finish/pallas_call | solution.py:252
